TPU v7x, 32 devices: a whole 2x2x4 slice. The times are simulated.
32 devices in a mesh: prompt: 4 (over z), sample: 4 (over x, core), vocab: 2 (over y).
Axes of the slice: x: 2, y: 2, z: 4, core: 2. Of those that a mesh axis runs over, the one named last changes fastest.
Arguments:
- hidden: bfloat16 [4, 24, 3584], P('sample', ('prompt', 'vocab')), may hold values from -170 to 170
- unembed: bfloat16 [152064, 3584], P(('prompt', 'vocab')), may hold values from -1 to 1
- token_ids: int32 [4, 24], P('sample', ('prompt', 'vocab')), may hold values from 0 to 152063, as said below
- old_logp: float32 [4, 24], P('sample', ('prompt', 'vocab')), may hold values from -14 to -11
- ref_logp: float32 [4, 24], P('sample', ('prompt', 'vocab')), may hold values from -14 to -11
- loss_mask: int32 [4, 24], P('sample', ('prompt', 'vocab')), may hold values 0 or 1
- lengths: int32 [4, 4], P('prompt', 'sample'), may hold values from 1 to 6, as said below
- sample_valid: int32 [4, 4], P('prompt', 'sample'), may hold values 0 or 1
- rewards: int32 [4, 4], P('prompt', 'sample'), may hold values from -300 to 300
Outputs:
- token_logp: float32 [4, 24], P('sample', ('prompt', 'vocab'))
- token_loss: float32 [4, 24], P('sample', ('prompt', 'vocab'))
- advantages: float32 [4, 4], P('prompt', 'sample')
- loss: float32 [], replicated
Inputs may be any that keep to these rules, and one draw needn't show every extreme that they name: `token_ids`: token ids name vocabulary entries. `lengths`: some response in every draw has length 6.
All inputs are finite; a program needn't handle non-finite values. No bound on the sum of `loss_mask` or of `sample_valid` on one device may be relied on, other than what follows from the above.
Results may differ from a plain program's by a relative error of at most 0.0003.
Values may be sent and summed in bfloat16 or wider, within the bound.
A program may use at most 192 MiB of HBM per device.

v0:
```python
import jax
import jax.numpy as jnp
from jax import lax
from jax.sharding import PartitionSpec as P

clip_low = 0.8
clip_high = 1.2
dual_clip = 3.0
kl_weight = 0.04
reward_unit = 0.01
std_floor = 0.5


def combined_all(value, axis, join):
    pieces = jax.tree.map(lambda part: lax.all_gather(part, axis), value)
    head = jax.tree.map(lambda part: part[0], pieces)
    tail = jax.tree.map(lambda part: part[1:], pieces)
    total, _ = lax.scan(lambda total, slab: (join(total, slab), None), head, tail)
    return total


def shard_stats(row_block, labels, weight, vocab_start):
    logits = lax.dot_general(
        row_block, weight, (((1,), (1,)), ((), ())), preferred_element_type=jnp.float32
    )
    local_peak = jnp.max(logits, axis=1)
    exp_total = jnp.sum(jnp.exp(logits - local_peak[:, None]), axis=1)
    column = vocab_start + lax.broadcasted_iota(jnp.int32, logits.shape, 1)
    target = jnp.sum(jnp.where(column == labels[:, None], logits, 0.0), axis=1)
    return (local_peak, exp_total, target)


def merge_pairs(first_part, second_part):
    peak_one, total_one, target_one = first_part
    peak_two, total_two, target_two = second_part
    joined_peak = jnp.maximum(peak_one, peak_two)
    joined_total = total_one * jnp.exp(peak_one - joined_peak) + total_two * jnp.exp(
        peak_two - joined_peak
    )
    return (joined_peak, joined_total, target_one + target_two)


def local(
    hidden, unembed, token_ids, old_logp, ref_logp, loss_mask, lengths, sample_valid, rewards
):
    samples, local_rows, width = hidden.shape
    vocab_rows = unembed.shape[0]
    vocab_start = lax.axis_index(("prompt", "vocab")) * vocab_rows
    positions = lax.axis_index("vocab") * local_rows + lax.broadcasted_iota(
        jnp.int32, (samples, local_rows), 1
    )
    live_rows = (loss_mask == 1) & (positions < lengths.T) & (sample_valid.T == 1)
    live_float = live_rows.astype(jnp.float32)
    valid_f = sample_valid.astype(jnp.float32)
    scores = rewards.astype(jnp.float32) * reward_unit
    group_count, first_moment, second_moment = lax.psum(
        (
            jnp.sum(valid_f, axis=1),
            jnp.sum(valid_f * scores, axis=1),
            jnp.sum(valid_f * scores * scores, axis=1),
        ),
        "sample",
    )
    safe_count = jnp.maximum(group_count, 1.0)
    group_mean = first_moment / safe_count
    spread = jnp.sqrt(jnp.maximum(second_moment / safe_count - group_mean * group_mean, 0.0))
    advantages = valid_f * (scores - group_mean[:, None]) / jnp.maximum(spread, std_floor)[:, None]
    part_hidden = lax.all_gather(hidden, ("prompt", "vocab"), axis=1, tiled=True)
    part_ids = lax.all_gather(token_ids, ("prompt", "vocab"), axis=1, tiled=True)
    piece_rows = part_hidden.shape[1]
    piece_stats = shard_stats(
        part_hidden.reshape(samples * piece_rows, width),
        part_ids.reshape(samples * piece_rows),
        unembed,
        vocab_start,
    )
    peak_new = piece_stats[0].reshape(samples, piece_rows)
    total_new = piece_stats[1].reshape(samples, piece_rows)
    target_new = piece_stats[2].reshape(samples, piece_rows)
    row_top, total_all, target_all = combined_all(
        (peak_new, total_new, target_new), ("prompt", "vocab"), merge_pairs
    )
    own_start = lax.axis_index(("prompt", "vocab")) * local_rows

    def own_rows(values):
        return lax.dynamic_slice_in_dim(values, own_start, local_rows, 1)

    raw_logp = own_rows(target_all) - (own_rows(row_top) + jnp.log(own_rows(total_all)))
    token_logp = jnp.where(live_rows, raw_logp, 0.0)
    adv_rows = advantages.T
    prob_ratio = jnp.exp(raw_logp - old_logp)
    gain_side = adv_rows * jnp.minimum(prob_ratio, clip_high)
    loss_side = jnp.maximum(adv_rows * jnp.maximum(prob_ratio, clip_low), dual_clip * adv_rows)
    objective = jnp.where(adv_rows >= 0.0, gain_side, loss_side)
    log_gap = ref_logp - raw_logp
    kl_term = jnp.exp(log_gap) - log_gap - 1.0
    token_loss = jnp.where(live_rows, kl_weight * kl_term - objective, 0.0)
    loss_part = jnp.sum(token_loss)
    loss_total, live_total = lax.psum(
        (loss_part, jnp.sum(live_float)), ("prompt", "sample", "vocab")
    )
    loss = loss_total / jnp.maximum(live_total, 1.0)
    return (token_logp, token_loss, advantages, loss)


def solution(mesh):
    in_specs = (
        P("sample", ("prompt", "vocab"), None),
        P(("prompt", "vocab"), None),
        P("sample", ("prompt", "vocab")),
        P("sample", ("prompt", "vocab")),
        P("sample", ("prompt", "vocab")),
        P("sample", ("prompt", "vocab")),
        P("prompt", "sample"),
        P("prompt", "sample"),
        P("prompt", "sample"),
    )
    out_specs = (
        P("sample", ("prompt", "vocab")),
        P("sample", ("prompt", "vocab")),
        P("prompt", "sample"),
        P(),
    )
    return jax.shard_map(local, mesh=mesh, in_specs=in_specs, out_specs=out_specs, check_vma=False)
```

profile of v0, /device:TPU:12, one launch (start us, length us, event | category | flops | bytes accessed | tf_op | source)
XLA Modules:
  0.0 173.8 jit_solution(1254609279268593562)
XLA Ops:
  1.9 1.3 convert_reduce_fusion
  3.9 9.1 %all-reduce.6 = (f32[1]{0:T(128)}, f32[1]{0:T(128)}, f32[1]{0:T(128)}) all-reduce(f32[1]{0:T(128)} %bitcast.11, f32[1]{0:T(128)} %bitcast.12, f32[1]{0:T(128)} %bitcast.14), channel_id=1, replica_groups=mesh['prompt'=4,'sample'=4,'vocab'=2] {'sample'}, use_global_device_ids=true, to_apply=%region_5.0 | all-reduce | flops 3 | bytes 24 | tf_op jit(solution)/shard_map/psum | solution.py:56
  15.0 0.8 copy.14
  15.8 28.5 %all_gather.15 = bf16[1,24,3584]{2,0,1:T(2,128)(2,1)S(1)} all-gather(bf16[1,3,3584]{2,0,1:T(2,128)(2,1)S(1)} %copy.14), channel_id=1, replica_groups=mesh['prompt'=4,'sample'=4,'vocab'=2] {'prompt','vocab'}, dimensions={1}, use_global_device_ids=true | all-gather | bytes 193536 | tf_op jit(solution)/shard_map/all_gather | solution.py:68
  44.3 0.0 copy-start.3
  44.3 0.0 copy-start.2
  44.3 48.0 %fusion.21 = (f32[24]{0:T(128)S(1)}, f32[24,19008]{1,0:T(8,128)S(1)}) fusion(bf16[19008,3584]{1,0:T(8,128)(2,1)} %param.12, bf16[1,24,3584]{2,0,1:T(2,128)(2,1)S(1)} %all_gather.15), kind=kOutput, calls=%fused_computation.36 | convolution fusion | flops 3270440448 | bytes 138246240 | tf_op jit(solution)/shard_map/dot_general | solution.py:23
  92.3 0.0 copy-start
  92.3 0.0 copy-start.1
  92.3 0.0 copy-done.3
  92.3 0.6 dynamic-slice
  93.6 0.2 dynamic-update-slice
  94.5 0.0 copy-done.2
  94.5 0.1 bitcast_dynamic-update-slice_fusion
  94.6 11.2 %all-reduce.2 = s32[24]{0:T(128)S(1)} all-reduce(s32[24]{0:T(128)S(1)} %bitcast_dynamic-update-slice_fusion), channel_id=1, replica_groups=mesh['prompt'=4,'sample'=4,'vocab'=2] {'prompt','vocab'}, use_global_device_ids=true, to_apply=%add.2 | all-reduce | flops 24 | bytes 192
  105.8 0.7 select_reduce_fusion
  106.6 0.2 dynamic-update-slice.1
  106.8 0.2 dynamic-update-slice.3
  107.0 17.1 %all-reduce.5 = (f32[192]{0:T(256)S(1)}, f32[192]{0:T(256)S(1)}, f32[192]{0:T(256)S(1)}) all-reduce(f32[192]{0:T(256)S(1)} %dynamic-update-slice, f32[192]{0:T(256)S(1)} %dynamic-update-slice.1, f32[192]{0:T(256)S(1)} %dynamic-update-slice.3), channel_id=2, replica_groups=mesh['prompt'=4,'sample'=4,'vocab'=2] {'prompt','vocab'}, use_global_device_ids=true, to_apply=%add | all-reduce | flops 576 | bytes 4608
  124.1 0.1 slice.27
  124.2 0.1 reshape.48
  124.3 0.1 slice.28
  124.4 0.1 reshape.49
  124.5 0.1 slice.29
  124.5 0.1 reshape.50
  124.6 0.3 while.14
  124.9 0.0 copy-done
  124.9 0.0 copy-done.1
  124.9 1.2 fusion.18
  126.1 0.5 broadcast_select_fusion.1
  126.6 43.7 %all-reduce.4 = (f32[]{:T(128)}, f32[]{:T(128)}) all-reduce(f32[]{:T(128)} %get-tuple-element.74, f32[]{:T(128)} %get-tuple-element.72), channel_id=1, replica_groups=mesh['prompt'=4,'sample'=4,'vocab'=2] {'prompt','sample','vocab'}, use_global_device_ids=true, to_apply=%region_9.10 | all-reduce | flops 2 | bytes 16 | tf_op jit(solution)/shard_map/psum | solution.py:99
  (14 shorter events, 0.2 us)
Async XLA Ops:
  44.3 48.0 %copy-start.3 = (u32[32]{0:T(128)S(1)}, u32[32]{0:T(128)}, u32[]{:S(2)}) copy-start(u32[32]{0:T(128)} %constant.69) | copy-start | bytes 388
  44.3 50.2 %copy-start.2 = (s32[1,3]{1,0:T(1,128)S(1)}, s32[1,3]{1,0:T(1,128)}, u32[]{:S(2)}) copy-start(s32[1,3]{1,0:T(1,128)} %param.13) | copy-start | bytes 40
  92.3 32.6 %copy-start = (f32[1,3]{1,0:T(1,128)S(1)}, f32[1,3]{1,0:T(1,128)}, u32[]{:S(2)}) copy-start(f32[1,3]{1,0:T(1,128)} %param.14) | copy-start | bytes 40
  92.3 32.6 %copy-start.1 = (f32[1,3]{1,0:T(1,128)S(1)}, f32[1,3]{1,0:T(1,128)}, u32[]{:S(2)}) copy-start(f32[1,3]{1,0:T(1,128)} %param.15) | copy-start | bytes 40
where the time goes:
time: 174 us
  blocking collectives  110 us (63%)
  matrix products  48 us (28%)
  between operations  9.57 us (6%)
  other arithmetic  3.97 us (2%)
  local copies, waits for them, and re-layouts  2.71 us (2%)
    dot_general x1, matrix products, shard_stats(): lax.dot_general(row_block, weight, (((1,), (1,)), ((), ())), preferred_el...  48 us
    psum x1, blocking collectives, local(): lax.psum((loss_part, jnp.sum(live_float)), ('prompt', 'sample', 'vocab'))  43.7 us
    all_gather x1, blocking collectives, local(): lax.all_gather(hidden, ('prompt', 'vocab'), axis=1, tiled=True)  28.5 us
    unnamed x2, blocking collectives  28.4 us
    psum x1, blocking collectives, local(): lax.psum((jnp.sum(valid_f, axis=1), jnp.sum(valid_f * scores, axis=1), jn...  9.06 us

commit v1 on v0

--- a/solution.py
+++ b/solution.py
@@ -97,7 +97,7 @@
     token_loss = jnp.where(live_rows, kl_weight * kl_term - objective, 0.0)
     loss_part = jnp.sum(token_loss)
     loss_total, live_total = lax.psum(
-        (loss_part, jnp.sum(live_float)), ("prompt", "sample", "vocab")
+        lax.psum((loss_part, jnp.sum(live_float)), "prompt"), ("sample", "vocab")
     )
     loss = loss_total / jnp.maximum(live_total, 1.0)
     return (token_logp, token_loss, advantages, loss)

time: 174 us -> 159 us (0.914)
  blocking collectives: 110 us -> 92.9 us
    psum x1 -> x2, blocking collectives: 43.7 us -> 27 us  [the longest x1 14.9 us: local(): lax.psum(lax.psum((loss_part, jnp.sum(live_float)), 'prompt'), ('sample',...]
where the time goes in v1:
time: 159 us; the launch traced here: 157 us
  blocking collectives  92.9 us (58%)
  matrix products  48 us (30%)
  between operations  9.62 us (6%)
  other arithmetic  4 us (3%)
  local copies, waits for them, and re-layouts  2.71 us (2%)
    dot_general x1, matrix products, shard_stats(): lax.dot_general(row_block, weight, (((1,), (1,)), ((), ())), preferred_el...  48 us
    all_gather x1, blocking collectives, local(): lax.all_gather(hidden, ('prompt', 'vocab'), axis=1, tiled=True)  28.5 us
    unnamed x2, blocking collectives  28.4 us
    psum x1, blocking collectives, local(): lax.psum(lax.psum((loss_part, jnp.sum(live_float)), 'prompt'), ('sample',...  14.9 us
    psum x1, blocking collectives, local(): lax.psum((loss_part, jnp.sum(live_float)), 'prompt')  12.2 us
    psum x1, blocking collectives, local(): lax.psum((jnp.sum(valid_f, axis=1), jnp.sum(valid_f * scores, axis=1), jn...  9.01 us

profile of v1, /device:TPU:12, one launch (start us, length us, event | category | flops | bytes accessed | tf_op | source)
XLA Modules:
  0.0 157.3 jit_solution(12646879372017633839)
XLA Ops:
  1.9 1.3 convert_reduce_fusion
  3.9 9.0 %all-reduce.6 = (f32[1]{0:T(128)}, f32[1]{0:T(128)}, f32[1]{0:T(128)}) all-reduce(f32[1]{0:T(128)} %bitcast.11, f32[1]{0:T(128)} %bitcast.12, f32[1]{0:T(128)} %bitcast.14), channel_id=1, replica_groups=mesh['prompt'=4,'sample'=4,'vocab'=2] {'sample'}, use_global_device_ids=true, to_apply=%region_5.0 | all-reduce | flops 3 | bytes 24 | tf_op jit(solution)/shard_map/psum | solution.py:56
  15.0 0.8 copy.14
  15.8 28.5 %all_gather.15 = bf16[1,24,3584]{2,0,1:T(2,128)(2,1)S(1)} all-gather(bf16[1,3,3584]{2,0,1:T(2,128)(2,1)S(1)} %copy.14), channel_id=1, replica_groups=mesh['prompt'=4,'sample'=4,'vocab'=2] {'prompt','vocab'}, dimensions={1}, use_global_device_ids=true | all-gather | bytes 193536 | tf_op jit(solution)/shard_map/all_gather | solution.py:68
  44.3 0.0 copy-start.3
  44.3 0.0 copy-start.2
  44.3 48.0 %fusion.21 = (f32[24]{0:T(128)S(1)}, f32[24,19008]{1,0:T(8,128)S(1)}) fusion(bf16[19008,3584]{1,0:T(8,128)(2,1)} %param.12, bf16[1,24,3584]{2,0,1:T(2,128)(2,1)S(1)} %all_gather.15), kind=kOutput, calls=%fused_computation.36 | convolution fusion | flops 3270440448 | bytes 138246240 | tf_op jit(solution)/shard_map/dot_general | solution.py:23
  92.2 0.0 copy-start
  92.2 0.0 copy-start.1
  92.3 0.0 copy-done.3
  92.3 0.6 dynamic-slice
  93.5 0.2 dynamic-update-slice
  94.4 0.0 copy-done.2
  94.4 0.1 bitcast_dynamic-update-slice_fusion
  94.5 11.2 %all-reduce.2 = s32[24]{0:T(128)S(1)} all-reduce(s32[24]{0:T(128)S(1)} %bitcast_dynamic-update-slice_fusion), channel_id=1, replica_groups=mesh['prompt'=4,'sample'=4,'vocab'=2] {'prompt','vocab'}, use_global_device_ids=true, to_apply=%add.2 | all-reduce | flops 24 | bytes 192
  105.8 0.7 select_reduce_fusion
  106.5 0.2 dynamic-update-slice.1
  106.8 0.2 dynamic-update-slice.3
  107.0 17.1 %all-reduce.5 = (f32[192]{0:T(256)S(1)}, f32[192]{0:T(256)S(1)}, f32[192]{0:T(256)S(1)}) all-reduce(f32[192]{0:T(256)S(1)} %dynamic-update-slice, f32[192]{0:T(256)S(1)} %dynamic-update-slice.1, f32[192]{0:T(256)S(1)} %dynamic-update-slice.3), channel_id=2, replica_groups=mesh['prompt'=4,'sample'=4,'vocab'=2] {'prompt','vocab'}, use_global_device_ids=true, to_apply=%add | all-reduce | flops 576 | bytes 4608
  124.1 0.1 slice.27
  124.2 0.1 reshape.48
  124.2 0.1 slice.28
  124.3 0.1 reshape.49
  124.4 0.1 slice.29
  124.5 0.1 reshape.50
  124.6 0.3 while.14
  124.8 0.0 copy-done
  124.9 0.0 copy-done.1
  124.9 1.2 fusion.18
  126.1 0.5 broadcast_select_fusion.1
  126.6 12.2 %all-reduce.7 = (f32[]{:T(128)}, f32[]{:T(128)}) all-reduce(f32[]{:T(128)} %get-tuple-element.76, f32[]{:T(128)} %get-tuple-element.74), channel_id=1, replica_groups=mesh['prompt'=4,'sample'=4,'vocab'=2] {'prompt'}, use_global_device_ids=true, to_apply=%region_9.10 | all-reduce | flops 2 | bytes 16 | tf_op jit(solution)/shard_map/psum | solution.py:100
  138.8 14.9 %all-reduce.4 = (f32[]{:T(128)}, f32[]{:T(128)}) all-reduce(f32[]{:T(128)} %get-tuple-element.70, f32[]{:T(128)} %get-tuple-element.71), channel_id=1, replica_groups=mesh['prompt'=4,'sample'=4,'vocab'=2] {'sample','vocab'}, use_global_device_ids=true, to_apply=%region_10.11 | all-reduce | flops 2 | bytes 16 | tf_op jit(solution)/shard_map/psum | solution.py:99
  (14 shorter events, 0.2 us)
Async XLA Ops:
  44.3 48.0 %copy-start.3 = (u32[32]{0:T(128)S(1)}, u32[32]{0:T(128)}, u32[]{:S(2)}) copy-start(u32[32]{0:T(128)} %constant.69) | copy-start | bytes 388
  44.3 50.2 %copy-start.2 = (s32[1,3]{1,0:T(1,128)S(1)}, s32[1,3]{1,0:T(1,128)}, u32[]{:S(2)}) copy-start(s32[1,3]{1,0:T(1,128)} %param.13) | copy-start | bytes 40
  92.2 32.6 %copy-start = (f32[1,3]{1,0:T(1,128)S(1)}, f32[1,3]{1,0:T(1,128)}, u32[]{:S(2)}) copy-start(f32[1,3]{1,0:T(1,128)} %param.14) | copy-start | bytes 40
  92.2 32.6 %copy-start.1 = (f32[1,3]{1,0:T(1,128)S(1)}, f32[1,3]{1,0:T(1,128)}, u32[]{:S(2)}) copy-start(f32[1,3]{1,0:T(1,128)} %param.15) | copy-start | bytes 40
